TPU v7x, 512 devices: a whole 4x8x8 slice. The times are simulated.
512 devices in a mesh: kgrp: 128 (over y, x, z_hi), img: 4 (over z_lo, core).
Axes of the slice: x: 4, y: 8, z: 8 (z_hi: 4, z_lo: 2; z = z_hi * 2 + z_lo), core: 2. Of those that a mesh axis runs over, the one named last changes fastest.
Arguments:
- vectors: float32 [2, 16, 16384], P(None, 'img', 'kgrp'), may hold values from -6 to 6
- conduction: bfloat16 [256, 2, 8, 4, 4096], P('kgrp', None, None, 'img'), may hold values from -6 to 6
- valence: bfloat16 [256, 2, 8, 4, 4096], P('kgrp', None, None, 'img'), may hold values from -6 to 6
- hole_point: int32 [1], replicated, may hold values from 0 to 16383
- kpoint_grid: int32 [3, 256], replicated, may hold values from 0 to 11
- image_cells: int32 [3, 512], replicated, may hold values from -6 to 6
Outputs:
- psi_real: float32 [16, 4, 4096, 512], P(None, 'img', 'kgrp')
- psi_imag: float32 [16, 4, 4096, 512], P(None, 'img', 'kgrp')
All inputs are finite; a program needn't handle non-finite values.
Results may differ from a plain program's by a relative error of at most 0.0043.
Values may be sent and summed in bfloat16 or wider, within the bound.
A program may use at most 64 MiB of HBM per device.

v0:
```python
import jax
import jax.numpy as jnp
import numpy as np
from jax import lax
from jax.sharding import PartitionSpec as P

NV = 8
NC = 8


cosine_levels = np.cos(2.0 * np.pi * np.arange(12) / 12.0)
sine_levels = np.sin(2.0 * np.pi * np.arange(12) / 12.0)


def phase_table(kpoint_grid, image_cells):
    turn_count = kpoint_grid[0][:, None] * image_cells[0][None, :]
    turn_count = turn_count + kpoint_grid[1][:, None] * image_cells[1][None, :]
    turn_count = turn_count + kpoint_grid[2][:, None] * image_cells[2][None, :]
    turn_count = jnp.mod(turn_count, 12)
    cosine = jnp.zeros(turn_count.shape, jnp.float32)
    sine_part = jnp.zeros(turn_count.shape, jnp.float32)
    for level_index in range(12):
        matches = turn_count == level_index
        cosine = jnp.where(matches, jnp.float32(cosine_levels[level_index]), cosine)
        sine_part = jnp.where(matches, jnp.float32(sine_levels[level_index]), sine_part)
    upper_half = jnp.stack([cosine, sine_part], 1)
    lower_half = jnp.stack([-sine_part, cosine], 1)
    return jnp.stack([upper_half, lower_half], 0).astype(jnp.bfloat16)


def hole_weights(amplitudes, hole_values):
    norm_factor = (NV * NC) ** (-0.5)
    real_amplitude = amplitudes[0]
    imaginary_amplitude = amplitudes[1]
    real_hole = hole_values[:, 0]
    imaginary_hole = hole_values[:, 1]
    highest = lax.Precision.HIGHEST
    weight_real = jnp.einsum("skvc,kv->ksc", real_amplitude, real_hole, precision=highest)
    weight_real = weight_real + jnp.einsum(
        "skvc,kv->ksc", imaginary_amplitude, imaginary_hole, precision=highest
    )
    weight_imaginary = jnp.einsum("skvc,kv->ksc", imaginary_amplitude, real_hole, precision=highest)
    weight_imaginary = weight_imaginary - jnp.einsum(
        "skvc,kv->ksc", real_amplitude, imaginary_hole, precision=highest
    )
    return jnp.stack([weight_real * norm_factor, weight_imaginary * norm_factor], 1).astype(
        jnp.bfloat16
    )


def mixing(weights):
    weight_real = weights[:, 0]
    weight_imaginary = weights[:, 1]
    first_row = jnp.stack([weight_real, -weight_imaginary], 2)
    second_row = jnp.stack([weight_imaginary, weight_real], 2)
    return jnp.stack([first_row, second_row], 1)


def shards(vectors, conduction, valence, hole_point, kpoint_grid, image_cells):
    group_size = lax.axis_size("kgrp")
    local_k = conduction.shape[0]
    slab_width = conduction.shape[4]
    own_excitons = vectors.shape[1]
    blocks = vectors.shape[2] // group_size
    columns = vectors.reshape(2, own_excitons, group_size, blocks)
    owned_columns = lax.all_to_all(columns, "kgrp", split_axis=2, concat_axis=2, tiled=True)
    owned_columns = owned_columns.reshape(2, own_excitons, local_k, NV, NC)
    hole_offset = hole_point[0] % slab_width
    hole_slab = hole_point[0] // slab_width
    present = (lax.axis_index("img") == hole_slab).astype(jnp.float32)
    picked = (
        lax.dynamic_slice_in_dim(valence[:, :, :, 0, :], hole_offset, 1, 3)[..., 0].astype(
            jnp.float32
        )
        * present
    )
    hole_values = lax.psum(picked, "img")
    all_columns = lax.all_gather(owned_columns, "img", axis=1, tiled=True)
    weights = hole_weights(all_columns, hole_values)
    phases = phase_table(kpoint_grid, image_cells)
    products = jnp.einsum(
        "kasbc,kbcp->sakp",
        mixing(weights),
        conduction[:, :, :, 0, :],
        preferred_element_type=jnp.float32,
    ).astype(jnp.bfloat16)
    summed = jnp.einsum(
        "sakp,akbn->spbn",
        lax.all_to_all(products, "kgrp", split_axis=3, concat_axis=2, tiled=True),
        phases,
        preferred_element_type=jnp.float32,
    )
    normal_scale = (2 * kpoint_grid.shape[1]) ** (-0.5)
    summed = summed * normal_scale
    return (summed[:, None, :, 0, :], summed[:, None, :, 1, :])


def solution(mesh):
    placed = (
        P(None, "img", "kgrp"),
        P("kgrp", None, None, "img", None),
        P("kgrp", None, None, "img", None),
        P(),
        P(),
        P(),
    )
    return jax.shard_map(
        shards,
        mesh=mesh,
        in_specs=placed,
        out_specs=(P(None, "img", "kgrp", None), P(None, "img", "kgrp", None)),
        check_vma=False,
    )
```

profile of v0, /device:TPU:1, one launch (start us, length us, event | category | flops | bytes accessed | tf_op | source)
XLA Modules:
  0.0 111.6 jit_solution(5236022632202495821)
XLA Ops:
  0.6 0.0 copy-start
  0.6 1.5 %copy.29 = f32[2,4,128]{1,0,2:T(2,128)} copy(f32[2,4,128]{2,1,0:T(4,128)} %param.6) | data formatting | bytes 8192 | tf_op args[0]
  2.2 20.8 %all-to-all-start = ((f32[2,4,128,1]{1,0,3,2:T(2,128)}), f32[2,4,128,1]{1,0,3,2:T(2,128)S(1)}, u32[]{:S(2)}, u32[]{:S(2)}) async-start(f32[2,4,128,1]{1,0,3,2:T(2,128)} %bitcast.4), calls=%async_computation | async-start | bytes 262144 | tf_op jit(solution)/shard_map/all_to_all | solution.py:66
  23.7 0.9 multiply_reduce_fusion
  24.5 6.0 %psum.7 = f32[2,2,8]{2,1,0:T(2,128)S(1)} all-reduce(f32[2,2,8]{2,1,0:T(2,128)S(1)} %multiply_reduce_fusion), channel_id=1, replica_groups=mesh['kgrp'=128,'img'=4] {'img'}, use_global_device_ids=true, to_apply=%region_0.1 | all-reduce | flops 32 | bytes 256 | tf_op jit(solution)/shard_map/psum | solution.py:77
  30.5 6.1 %all-to-all-done = f32[2,4,128,1]{1,0,3,2:T(2,128)S(1)} async-done(((f32[2,4,128,1]{1,0,3,2:T(2,128)}), f32[2,4,128,1]{1,0,3,2:T(2,128)S(1)}, u32[]{:S(2)}, u32[]{:S(2)}) %all-to-all-start) | async-done | bytes 4128 | tf_op jit(solution)/shard_map/all_to_all | solution.py:66
  36.6 0.3 copy.30
  36.9 7.7 %all_gather.3 = f32[2,16,2,8,8]{4,3,2,0,1:T(8,128)S(1)} all-gather(f32[2,4,2,8,8]{4,3,2,0,1:T(8,128)S(1)} %copy.30), channel_id=1, replica_groups=mesh['kgrp'=128,'img'=4] {'img'}, dimensions={1}, use_global_device_ids=true | all-gather | bytes 20480 | tf_op jit(solution)/shard_map/all_gather | solution.py:78
  44.7 0.3 fusion.15
  44.9 0.3 fusion.13
  45.2 0.3 fusion.19
  45.4 0.3 fusion.17
  45.7 0.1 copy.41
  45.8 0.1 copy.44
  45.8 0.1 copy.45
  45.9 0.1 copy.46
  46.0 0.0 copy-done
  46.0 0.3 fusion.1
  46.4 7.1 %copy.32 = bf16[16,2,2,4096]{0,1,2,3:T(2,128)(2,1)} copy(bf16[16,2,2,4096]{3,0,1,2:T(8,128)(2,1)S(1)} %fusion.1) | data formatting | bytes 1048576 | tf_op jit(solution)/shard_map/convert_element_type | solution.py:86
  53.5 0.0 copy-start.2
  53.5 0.0 copy-start.1
  53.5 12.9 %reshape.653 = bf16[128,2,1024]{2,1,0:T(2,128)(2,1)} reshape(bf16[4096,2,2,16]{3,2,1,0:T(2,128)(2,1)} %bitcast.114) | data formatting | bytes 1048576
  66.4 8.8 %all-to-all-start.1 = ((bf16[128,2,1024]{2,1,0:T(2,128)(2,1)}), bf16[128,2,1024]{2,1,0:T(2,128)(2,1)S(1)}, u32[]{:S(2)}, u32[]{:S(2)}) async-start(bf16[128,2,1024]{2,1,0:T(2,128)(2,1)} %reshape.653), calls=%async_computation.1 | async-start | bytes 1048576 | tf_op jit(solution)/shard_map/all_to_all | solution.py:89
  75.2 0.0 copy-done.2
  75.2 0.0 copy-done.1
  75.2 1.1 fusion.12
  76.3 0.1 maximum_bitcast_fusion.2
  76.4 20.0 %all-to-all-done.1 = bf16[128,2,1024]{2,1,0:T(2,128)(2,1)S(1)} async-done(((bf16[128,2,1024]{2,1,0:T(2,128)(2,1)}), bf16[128,2,1024]{2,1,0:T(2,128)(2,1)S(1)}, u32[]{:S(2)}, u32[]{:S(2)}) %all-to-all-start.1) | async-done | bytes 524320 | tf_op jit(solution)/shard_map/all_to_all | solution.py:89
  96.4 4.1 %reshape.654 = bf16[4096,2,2,16]{3,2,1,0:T(2,128)(2,1)} reshape(bf16[128,2,1024]{2,1,0:T(2,128)(2,1)S(1)} %all-to-all-done.1) | data formatting | bytes 1048576
  100.6 8.6 %copy.52 = bf16[16,2,2,128,32]{4,0,2,3,1:T(8,128)(2,1)S(1)} copy(bf16[16,2,2,128,32]{0,1,2,4,3:T(2,128)(2,1)} %bitcast.115) | data formatting | bytes 1048576 | tf_op jit(solution)/shard_map/all_to_all | solution.py:89
  109.1 0.9 bitcast_multiply_fusion
  110.1 1.5 %slice_bitcast_fusion = (f32[16,1,32,512]{3,2,1,0:T(8,128)}, f32[16,1,32,512]{3,2,1,0:T(8,128)}) fusion(f32[16,32,2,512]{3,1,2,0:T(8,128)S(1)} %bitcast_multiply_fusion), kind=kLoop, calls=%fused_computation.6 | loop fusion | bytes 4194304
  (6 shorter events, 0.1 us)
Async XLA Ops:
  0.6 45.4 %copy-start = (bf16[2,2,8,1,4096]{4,2,3,1,0:T(8,128)(2,1)S(1)}, bf16[2,2,8,1,4096]{4,2,3,1,0:T(8,128)(2,1)}, u32[]{:S(2)}) copy-start(bf16[2,2,8,1,4096]{4,2,3,1,0:T(8,128)(2,1)} %param.7) | copy-start | bytes 786436
  2.2 34.4 %all-to-all-start = ((f32[2,4,128,1]{1,0,3,2:T(2,128)}), f32[2,4,128,1]{1,0,3,2:T(2,128)S(1)}, u32[]{:S(2)}, u32[]{:S(2)}) async-start(f32[2,4,128,1]{1,0,3,2:T(2,128)} %bitcast.4), calls=%async_computation | async-start | bytes 262144 | tf_op jit(solution)/shard_map/all_to_all | solution.py:66
  53.5 21.7 %copy-start.2 = (s32[3,256]{1,0:T(4,128)S(1)}, s32[3,256]{1,0:T(4,128)}, u32[]{:S(2)}) copy-start(s32[3,256]{1,0:T(4,128)} %param.10) | copy-start | bytes 9220
  53.5 21.7 %copy-start.1 = (s32[3,512]{1,0:T(4,128)S(1)}, s32[3,512]{1,0:T(4,128)}, u32[]{:S(2)}) copy-start(s32[3,512]{1,0:T(4,128)} %param.11) | copy-start | bytes 18436
  66.4 30.0 %all-to-all-start.1 = ((bf16[128,2,1024]{2,1,0:T(2,128)(2,1)}), bf16[128,2,1024]{2,1,0:T(2,128)(2,1)S(1)}, u32[]{:S(2)}, u32[]{:S(2)}) async-start(bf16[128,2,1024]{2,1,0:T(2,128)(2,1)} %reshape.653), calls=%async_computation.1 | async-start | bytes 1048576 | tf_op jit(solution)/shard_map/all_to_all | solution.py:89
where the time goes:
time: 112 us
  local copies, waits for them, and re-layouts  36.4 us (32%)
  starting transfers between devices  29.6 us (26%)
  waiting for transfers between devices  26.2 us (23%)
  blocking collectives  13.7 us (12%)
  matrix products  2.29 us (2%)
  other arithmetic  2.02 us (2%)
  between operations  1.47 us (1%)
    all_to_all x1, starting transfers between devices, shards(): lax.all_to_all(columns, 'kgrp', split_axis=2, concat_axis=2, tiled=True)  20.8 us
    unnamed x10, local copies, waits for them, and re-layouts  20.1 us
    all_to_all x1, waiting for transfers between devices, shards(): lax.all_to_all(products, 'kgrp', split_axis=3, concat_axis=2, tiled=True)  20 us
    all_to_all x1, starting transfers between devices, shards(): lax.all_to_all(products, 'kgrp', split_axis=3, concat_axis=2, tiled=True)  8.78 us
    all_to_all x1, local copies, waits for them, and re-layouts, shards(): lax.all_to_all(products, 'kgrp', split_axis=3, concat_axis=2, tiled=True)  8.56 us
    all_gather x1, blocking collectives, shards(): all_columns = lax.all_gather(owned_columns, 'img', axis=1, tiled=True)  7.73 us
    convert_element_type x1, local copies, waits for them, and re-layouts, shards(): products = jnp.einsum('kasbc,kbcp->sakp', mixing(weights), conduction[:,...  7.13 us
    all_to_all x1, waiting for transfers between devices, shards(): lax.all_to_all(columns, 'kgrp', split_axis=2, concat_axis=2, tiled=True)  6.13 us
  transfers between devices with their start and end apart: 2, of which 2 were waited for; matrix products, arithmetic and copies ran while one was open for 2% of the time, Pallas kernels for 0%

commit v1 on v0

v1 whole, which is shorter than its diff:
```python
import functools

import jax
import jax.numpy as jnp
import numpy as np
from jax import lax
from jax.experimental import pallas as pl
from jax.experimental.pallas import tpu as pltpu
from jax.sharding import PartitionSpec as P

MESH = pl.DeviceIdType.MESH
RING = (8, 4, 4)
NV = 8
NC = 8
LANES = 128
PTS = 32


def drain(sem, ref):
    pltpu.make_async_copy(ref, ref, sem).wait()


def exchange(
    ring,
    groups,
    nc,
    hole_ref,
    vec_ref,
    cond_hbm,
    val_hbm,
    ct_ref,
    wt_ref,
    cond_v,
    val_v,
    dest,
    cz,
    cx,
    cf,
    cs,
    vf,
    hi,
    hf,
    hs,
    wf,
    load_sem,
    cz_send,
    cz_recv,
    cx_send,
    cx_recv,
    cy_send,
    cy_recv,
    vy_send,
    vy_recv,
    vz_send,
    vz_recv,
    vx_send,
    vx_recv,
    hi_send,
    hi_recv,
    hy_send,
    hy_recv,
    hz_send,
    hz_recv,
    hx_send,
    hx_recv,
    w_send,
    w_recv,
):
    ny, nx, nz = ring
    count = ny * nx * nz
    me = lax.axis_index("kgrp")
    img = lax.axis_index("img")
    y = lax.div(me, nx * nz)
    x = lax.rem(lax.div(me, nz), nx)
    z = lax.rem(me, nz)

    def at(yy, xx, zz, gg):
        return ((yy * nx + xx) * nz + zz, gg)

    def y_peer(step):
        yy = lax.rem(y + step, ny)
        return yy, at(yy, x, z, img)

    def x_peer(step):
        xx = lax.rem(x + step, nx)
        return xx, at(y, xx, z, img)

    def z_peer(step):
        zz = lax.rem(z + step, nz)
        return zz, at(y, x, zz, img)

    def img_peer(step):
        return (me, lax.rem(img + step, groups))

    def send(src, dst, send_sem, recv_sem, device):
        pltpu.make_async_remote_copy(
            src_ref=src,
            dst_ref=dst,
            send_sem=send_sem,
            recv_sem=recv_sem,
            device_id=device,
            device_id_type=MESH,
        ).start()

    load_val = pltpu.make_async_copy(val_hbm, val_v, load_sem.at[0])
    load_cond = pltpu.make_async_copy(cond_hbm, cond_v, load_sem.at[1])
    load_val.start()
    load_cond.start()

    barrier = pltpu.get_barrier_semaphore()
    peers = (
        [y_peer(s)[1] for s in range(1, ny)]
        + [z_peer(s)[1] for s in range(1, nz)]
        + [x_peer(s)[1] for s in range(1, nx)]
        + [img_peer(s) for s in range(1, groups)]
    )
    for peer in peers:
        pl.semaphore_signal(barrier, inc=1, device_id=peer, device_id_type=MESH)

    vf[y, x, z] = vec_ref[...].reshape(8, vec_ref.shape[2]).astype(vf.dtype)

    points = val_v.shape[1]
    wanted = hole_ref[0] - img * points
    lane8 = lax.broadcasted_iota(jnp.int32, (8, LANES), 1)
    lane32 = lax.broadcasted_iota(jnp.int32, (32, LANES), 1)
    load_val.wait()

    def pick(j, kept):
        tile = val_v[:, pl.ds(pl.multiple_of(j * LANES, LANES), LANES)].astype(jnp.float32)
        return kept + jnp.where(lane32 + j * LANES == wanted, tile, 0.0)

    tile = lax.fori_loop(0, points // LANES, pick, jnp.zeros((32, LANES), jnp.float32))
    tile = jnp.concatenate([tile, jnp.zeros((LANES - 32, LANES), jnp.float32)], 0)
    tile = tile.astype(jnp.bfloat16)
    chosen = jnp.ones((8, LANES), jnp.bfloat16)
    row = lax.dot_general(
        chosen, tile, (((1,), (1,)), ((), ())), preferred_element_type=jnp.float32
    )
    hi[img] = row[0:1]

    load_cond.wait()
    low = lane8 < 64
    odd = lax.rem(lax.div(lane8, 32), 2) == 1

    def relay(j, carry):
        yy = lax.div(j, nx)
        xx = lax.rem(j, nx)
        t = [
            cond_v[q, :, pl.ds(pl.multiple_of(j * LANES, LANES), LANES)].astype(jnp.float32)
            for q in range(4)
        ]
        halves = []
        for q in range(2):
            halves.append(jnp.where(low, t[q], pltpu.roll(t[q + 2], 64, 1)))
        for q in range(2):
            halves.append(jnp.where(low, pltpu.roll(t[q], 64, 1), t[q + 2]))
        for h in range(2):
            first, second = halves[2 * h], halves[2 * h + 1]
            dest[yy, xx, 2 * h] = jnp.where(odd, pltpu.roll(second, 32, 1), first).astype(
                jnp.bfloat16
            )
            dest[yy, xx, 2 * h + 1] = jnp.where(odd, second, pltpu.roll(first, 96, 1)).astype(
                jnp.bfloat16
            )
        return carry

    lax.fori_loop(0, ny * nx, relay, 0)

    def own_z(j, carry):
        yy = lax.div(j, nx)
        xx = lax.rem(j, nx)
        cz[yy, z, xx] = dest[yy, xx, z]
        return carry

    lax.fori_loop(0, ny * nx, own_z, 0)

    pl.semaphore_wait(barrier, len(peers))

    for s in range(1, groups):
        send(hi.at[img], hi.at[img], hi_send, hi_recv, img_peer(s))
    far_y = sorted(range(1, ny), key=lambda s: -min(s, ny - s))
    far_z = sorted(range(1, nz), key=lambda s: -min(s, nz - s))
    far_x = sorted(range(1, nx), key=lambda s: -min(s, nx - s))
    for s in far_y:
        send(vf.at[y, x, z], vf.at[y, x, z], vy_send, vy_recv, y_peer(s)[1])

    order = far_y + [0]
    for s in order:
        yy = lax.rem(y + s, ny)
        for t in far_z:
            zz, device = z_peer(t)
            send(dest.at[yy, :, zz], cz.at[yy, z], cz_send, cz_recv.at[s], device)

    drain(hi_recv, hi.at[pl.ds(0, groups - 1)])
    total = hi[0]
    for s in range(1, groups):
        total = total + hi[s]
    hf[y, x, z] = total

    drain(vy_recv, vf.at[pl.ds(0, ny - 1), 0, 0])
    for t in far_z:
        send(vf.at[:, x, z], vf.at[:, x, z], vz_send, vz_recv.at[t], z_peer(t)[1])
    for t in far_x:
        send(vf.at[:, x, z], vf.at[:, x, z], vx_send, vx_recv, x_peer(t)[1])
    for s in far_y:
        send(hf.at[y, x, z], hf.at[y, x, z], hy_send, hy_recv, y_peer(s)[1])

    def forward_x(s):
        yy = lax.rem(y + s, ny)
        drain(cz_recv.at[s], cz.at[yy, pl.ds(0, nz - 1)])
        for t in far_x:
            xx, device = x_peer(t)
            send(cz.at[yy, :, xx], cx.at[yy, x], cx_send, cx_recv.at[s], device)
        for zz in range(nz):
            cx[yy, x, zz] = cz[yy, zz, x]

    for s in order[: ny // 2]:
        forward_x(s)

    for t in sorted(range(1, nz), key=lambda t: min(t, nz - t)):
        zz = lax.rem(z + nz - t, nz)
        drain(vz_recv.at[t], vf.at[:, 0, 0])
        for u in far_x:
            send(vf.at[:, x, zz], vf.at[:, x, zz], vx_send, vx_recv, x_peer(u)[1])

    drain(hy_recv, hf.at[pl.ds(0, ny - 1), 0, 0])
    for t in far_z:
        send(hf.at[:, x, z], hf.at[:, x, z], hz_send, hz_recv, z_peer(t)[1])

    for s in order[ny // 2 :]:
        forward_x(s)

    def forward_y(s):
        yy, device = y_peer(s)
        drain(cx_recv.at[s], cx.at[yy, pl.ds(0, nx - 1)])
        send(cx.at[yy], cf.at[y], cy_send, cy_recv, device)

    for s in far_y[: ny // 2]:
        forward_y(s)

    drain(hz_recv, hf.at[:, 0, pl.ds(0, nz - 1)])
    for t in far_x:
        send(hf.at[:, x], hf.at[:, x], hx_send, hx_recv, x_peer(t)[1])

    for s in far_y[ny // 2 :]:
        forward_y(s)
    drain(cx_recv.at[0], cx.at[y, pl.ds(0, nx - 1)])
    cf[y] = cx[y]

    drain(vx_recv, vf.at[:, pl.ds(0, nx - 1)])
    drain(hx_recv, hf.at[:, pl.ds(0, nx - 1)])

    for d in range(count):
        hs[pl.ds(d, 1), :] = hf[d // (nx * nz), d // nz % nx, d % nz]
    holes = jnp.transpose(hs[...])
    upper = lax.broadcasted_iota(jnp.int32, (8, vf.shape[4]), 0) < 4
    for a in range(2):
        for c in range(nc):
            along = None
            across = None
            for v in range(NV):
                d = (a * NV + v) * nc + c
                piece = vf[d // (nx * nz), d // nz % nx, d % nz].astype(jnp.float32)
                real = piece * holes[a * 16 + v : a * 16 + v + 1]
                imag = piece * holes[a * 16 + 8 + v : a * 16 + 9 + v]
                along = real if along is None else along + real
                across = imag if across is None else across + imag
            across = pltpu.roll(across, 4, 0)
            weight = (along + jnp.where(upper, across, -across)) * ((NV * NC) ** -0.5)
            wf[img, a * nc + c] = weight.astype(jnp.bfloat16)

    for s in range(1, groups):
        send(wf.at[img], wf.at[img], w_send, w_recv, img_peer(s))

    drain(cy_recv, cf.at[pl.ds(0, ny - 1)])
    cs[...] = cf[...].astype(jnp.float32).reshape(cs.shape)
    for c in range(8):
        ct_ref[c] = jnp.transpose(cs[pl.ds(c, count, 8), :])

    drain(w_recv, wf.at[pl.ds(0, groups - 1)])
    wt_ref[...] = wf[...].astype(jnp.float32)

    drain(hi_send, hi.at[pl.ds(0, groups - 1)])
    drain(vy_send, vf.at[pl.ds(0, ny - 1), 0, 0])
    drain(vz_send, vf.at[:, 0, pl.ds(0, nz - 1)])
    drain(vx_send, vf.at[:, pl.ds(0, nx - 1)])
    drain(hy_send, hf.at[pl.ds(0, ny - 1), 0, 0])
    drain(hz_send, hf.at[:, 0, pl.ds(0, nz - 1)])
    drain(hx_send, hf.at[:, pl.ds(0, nx - 1)])
    drain(cz_send, cz.at[:, pl.ds(0, nz - 1)])
    drain(cx_send, cx.at[:, pl.ds(0, nx - 1)])
    drain(cy_send, cf.at[pl.ds(0, ny - 1)])
    drain(w_send, wf.at[pl.ds(0, groups - 1)])


def run_exchange(ring, groups, nc, hole, vec, cond, val, vec_type=jnp.bfloat16):
    ny, nx, nz = ring
    count = ny * nx * nz
    lanes = vec.shape[2]
    bf16, f32 = jnp.bfloat16, jnp.float32
    dma = pltpu.SemaphoreType.DMA
    vmem = pl.BlockSpec(memory_space=pltpu.VMEM)
    anywhere = pl.BlockSpec(memory_space=pltpu.HBM)
    scratch = [
        pltpu.VMEM(cond.shape, bf16),
        pltpu.VMEM(val.shape, bf16),
        pltpu.VMEM((ny, nx, nz, 8, LANES), bf16),
        pltpu.VMEM((ny, nz, nx, 8, LANES), bf16),
        pltpu.VMEM((ny, nx, nz, 8, LANES), bf16),
        pltpu.VMEM((ny, nx, nz, 8, LANES), bf16),
        pltpu.VMEM((count * 8, LANES), f32),
        pltpu.VMEM((ny, nx, nz, 8, lanes), vec_type),
        pltpu.VMEM((groups, 1, LANES), f32),
        pltpu.VMEM((ny, nx, nz, 1, LANES), f32),
        pltpu.VMEM((count, LANES), f32),
        pltpu.VMEM((groups, 2 * nc, 8, lanes), bf16),
        dma((2,)),
        dma(()),
        dma((ny,)),
        dma(()),
        dma((ny,)),
        dma(()),
        dma(()),
        dma(()),
        dma(()),
        dma(()),
        dma((nz,)),
        dma(()),
        dma(()),
        dma(()),
        dma(()),
        dma(()),
        dma(()),
        dma(()),
        dma(()),
        dma(()),
        dma(()),
        dma(()),
        dma(()),
    ]
    return pl.pallas_call(
        functools.partial(exchange, ring, groups, nc),
        out_shape=(
            jax.ShapeDtypeStruct((8, LANES, count), f32),
            jax.ShapeDtypeStruct((groups, 2 * nc, 8, lanes), f32),
        ),
        in_specs=[pl.BlockSpec(memory_space=pltpu.SMEM), vmem, anywhere, anywhere],
        out_specs=(vmem, vmem),
        scratch_shapes=scratch,
        compiler_params=pltpu.CompilerParams(
            collective_id=0, has_side_effects=True, vmem_limit_bytes=24 * 1024 * 1024
        ),
        name="exchange",
    )(hole, vec, cond, val)


COS30 = float(np.float32(jnp.bfloat16(np.cos(np.pi / 6))))
FIT = np.linalg.solve(
    np.array([[1.0, 1.0, 1.0], [1.0, 4.0, 16.0], [1.0, 9.0, 81.0]]),
    np.array([0.5, COS30 / 2, 1.0 / 3]),
)


def cosine(level):
    u = jnp.abs(level - 6.0) - 3.0
    square = u * u
    return u * (float(FIT[0]) + square * (float(FIT[1]) + square * float(FIT[2])))


def combine(ct_ref, wt_ref, kpt_ref, cell_ref, real_ref, imag_ref, table, lhs):
    bf16, f32 = jnp.bfloat16, jnp.float32

    @pl.when(pl.program_id(0) == 0)
    def _():
        kpt = kpt_ref[...].astype(f32)
        cell = cell_ref[...].astype(f32)
        kpt = jnp.concatenate([kpt, jnp.zeros((5, kpt.shape[1]), f32)], 0).astype(bf16)
        cell = jnp.concatenate([cell, jnp.zeros((5, cell.shape[1]), f32)], 0).astype(bf16)
        rows = lax.broadcasted_iota(jnp.int32, (256, 256), 0)
        columns = lax.broadcasted_iota(jnp.int32, (256, 256), 1)
        source = 2 * jnp.bitwise_and(columns, 127) + jnp.right_shift(columns, 7)
        swap = jnp.where(rows == source, 1.0, 0.0).astype(bf16)
        kpt = jnp.dot(kpt, swap, preferred_element_type=f32)
        for a in range(2):
            part = jnp.transpose(kpt[:, a * 128 : a * 128 + 128]).astype(bf16)
            turns = jnp.dot(part, cell, preferred_element_type=f32)
            turns = turns - 12.0 * jnp.floor((turns + 0.5) * (1.0 / 12.0))
            cos = cosine(turns).astype(bf16)
            shifted = turns - 3.0
            sin = cosine(jnp.where(shifted < 0.0, shifted + 12.0, shifted)).astype(bf16)
            table[a * 256 : a * 256 + 128, 0:512] = cos
            table[a * 256 : a * 256 + 128, 512:1024] = sin
            table[a * 256 + 128 : a * 256 + 256, 0:512] = -sin
            table[a * 256 + 128 : a * 256 + 256, 512:1024] = cos

    for a in range(2):
        for half in range(2):
            reals = []
            imags = []
            for c in range(NC):
                start = a * 64 + half * 16
                reals.append(ct_ref[c, start : start + 16, :])
                imags.append(ct_ref[c, start + 32 : start + 48, :])
            for s in range(4):
                out_real = None
                out_imag = None
                for c in range(NC):
                    wr = wt_ref[0, a * NC + c, s : s + 1, :]
                    wi = wt_ref[0, a * NC + c, s + 4 : s + 5, :]
                    tr = wr * reals[c] - wi * imags[c]
                    ti = wr * imags[c] + wi * reals[c]
                    out_real = tr if out_real is None else out_real + tr
                    out_imag = ti if out_imag is None else out_imag + ti
                first = s * 32 + half * 16
                lhs[first : first + 16, a * 256 : a * 256 + 128] = out_real.astype(bf16)
                lhs[first : first + 16, a * 256 + 128 : a * 256 + 256] = out_imag.astype(bf16)

    scale = 512.0**-0.5
    for part, ref in ((0, real_ref), (1, imag_ref)):
        ref[...] = (
            jnp.dot(
                lhs[...],
                table[:, part * 512 : part * 512 + 512],
                preferred_element_type=f32,
            )
            * scale
        )


def run_combine(ct, wt, kpoint_grid, image_cells):
    f32 = jnp.float32
    groups = wt.shape[0]
    rows = 4 * PTS
    return pl.pallas_call(
        combine,
        grid=(groups,),
        out_shape=(
            jax.ShapeDtypeStruct((groups * rows, 512), f32),
            jax.ShapeDtypeStruct((groups * rows, 512), f32),
        ),
        in_specs=[
            pl.BlockSpec(ct.shape, lambda i: (0, 0, 0)),
            pl.BlockSpec((1,) + wt.shape[1:], lambda i: (i, 0, 0, 0)),
            pl.BlockSpec(kpoint_grid.shape, lambda i: (0, 0)),
            pl.BlockSpec(image_cells.shape, lambda i: (0, 0)),
        ],
        out_specs=(
            pl.BlockSpec((rows, 512), lambda i: (i, 0)),
            pl.BlockSpec((rows, 512), lambda i: (i, 0)),
        ),
        scratch_shapes=[
            pltpu.VMEM((512, 1024), jnp.bfloat16),
            pltpu.VMEM((rows, 512), jnp.bfloat16),
        ],
        compiler_params=pltpu.CompilerParams(vmem_limit_bytes=24 * 1024 * 1024),
        name="combine",
    )(ct, wt, kpoint_grid, image_cells)


def shards(vectors, conduction, valence, hole_point, kpoint_grid, image_cells):
    points = conduction.shape[4]
    cond = conduction.reshape(4, 8, points)
    val = valence.reshape(32, points)
    ct, wt = run_exchange(RING, lax.axis_size("img"), NC, hole_point, vectors, cond, val)
    real, imag = run_combine(ct, wt, kpoint_grid, image_cells)
    shape = (16, 1, PTS, 512)
    return real.reshape(shape), imag.reshape(shape)


def solution(mesh):
    placed = (
        P(None, "img", "kgrp"),
        P("kgrp", None, None, "img", None),
        P("kgrp", None, None, "img", None),
        P(),
        P(),
        P(),
    )
    return jax.shard_map(
        shards,
        mesh=mesh,
        in_specs=placed,
        out_specs=(P(None, "img", "kgrp", None), P(None, "img", "kgrp", None)),
        check_vma=False,
    )
```

time: 112 us -> 46.1 us (0.41)
  Pallas kernels: 0 us -> 42.6 us
  local copies, waits for them, and re-layouts: 36.4 us -> 1.93 us
  starting transfers between devices: 29.6 us -> 0 us
  waiting for transfers between devices: 26.2 us -> 0 us
  blocking collectives: 13.7 us -> 0 us
  matrix products: 2.29 us -> 0 us
  other arithmetic: 2.02 us -> 0 us
    pallas_call x0 -> x2, Pallas kernels: none -> 42.6 us  [the longest x1 38.6 us: run_exchange(): pl.pallas_call(functools.partial(exchange, ring, groups, nc), out_shape=(...]
    all_to_all x2 -> x0, starting transfers between devices: 29.6 us -> none  [the longest x1 20.8 us: shards(): lax.all_to_all(columns, 'kgrp', split_axis=2, concat_axis=2, tiled=True)]
    all_to_all x2 -> x0, waiting for transfers between devices: 26.2 us -> none  [the longest x1 20 us: shards(): lax.all_to_all(products, 'kgrp', split_axis=3, concat_axis=2, tiled=True)]
    unnamed x10, local copies, waits for them, and re-layouts: 20.1 us -> 1.93 us
    all_to_all x1 -> x0, local copies, waits for them, and re-layouts: 8.56 us -> none  [shards(): lax.all_to_all(products, 'kgrp', split_axis=3, concat_axis=2, tiled=True)]
    all_gather x1 -> x0, blocking collectives: 7.73 us -> none  [shards(): all_columns = lax.all_gather(owned_columns, 'img', axis=1, tiled=True)]
    convert_element_type x1 -> x0, local copies, waits for them, and re-layouts: 7.13 us -> none  [shards(): products = jnp.einsum('kasbc,kbcp->sakp', mixing(weights), conduction[:,...]
    psum x1 -> x0, blocking collectives: 5.97 us -> none  [shards(): hole_values = lax.psum(picked, 'img')]
  transfers between devices with their start and end apart: 2 -> 0, of which waited for: 2 -> 0; matrix products, arithmetic and copies ran while one was open for 2% -> 0% of each run, Pallas kernels for 0% -> 0%
where the time goes in v1:
time: 46.1 us; the launch traced here: 45.8 us
  Pallas kernels  42.6 us (92%)
  local copies, waits for them, and re-layouts  1.93 us (4%)
  between operations  1.33 us (3%)
    pallas_call x1, Pallas kernels, run_exchange(): pl.pallas_call(functools.partial(exchange, ring, groups, nc), out_shape=(...  38.6 us
    pallas_call x1, Pallas kernels, run_combine(): pl.pallas_call(combine, grid=(groups,), out_shape=(jax.ShapeDtypeStruct((...  4 us
    unnamed x10, local copies, waits for them, and re-layouts  1.93 us

profile of v1, /device:TPU:1, one launch (start us, length us, event | category | flops | bytes accessed | tf_op | source)
XLA Modules:
  0.0 45.8 jit_solution(8538816211231470904)
XLA Ops:
  0.6 0.0 copy-start.3
  1.3 0.0 copy-done.3
  1.3 0.0 copy-start
  1.3 0.9 %copy-done = bf16[2,2,8,1,4096]{4,2,3,1,0:T(8,128)(2,1)S(1)} copy-done((bf16[2,2,8,1,4096]{4,2,3,1,0:T(8,128)(2,1)S(1)}, bf16[2,2,8,1,4096]{4,2,3,1,0:T(8,128)(2,1)}, u32[]{:S(2)}) %copy-start) | copy-done | bytes 262168
  2.3 0.0 copy-start.1
  2.3 0.9 %copy-done.1 = bf16[2,2,8,1,4096]{4,2,3,1,0:T(8,128)(2,1)S(1)} copy-done((bf16[2,2,8,1,4096]{4,2,3,1,0:T(8,128)(2,1)S(1)}, bf16[2,2,8,1,4096]{4,2,3,1,0:T(8,128)(2,1)}, u32[]{:S(2)}) %copy-start.1) | copy-done | bytes 262168
  3.2 0.0 copy-start.2
  3.2 0.0 copy-start.4
  3.2 38.6 %exchange.1 = (f32[8,128,128]{2,1,0:T(8,128)S(1)}, f32[4,16,8,128]{3,2,1,0:T(8,128)S(1)}) custom-call(s32[1]{0:T(128)S(6)} %copy.10.hole_ref, f32[2,4,128]{2,1,0:T(4,128)S(1)} %copy-done.3, bf16[4,8,4096]{2,1,0:T(8,128)(2,1)S(1)} %bitcast.8, bf16[32,4096]{1,0:T(8,128)(2,1)S(1)} %bitcast.9), custom_call_target="tpu_custom_call" | custom-call | tf_op jit(solution)/shard_map/exchange/pallas_call | solution.py:341
  41.8 0.0 copy-done.2
  41.8 0.0 copy-done.4
  41.8 4.0 %combine.1 = (f32[512,512]{1,0:T(8,128)}, f32[512,512]{1,0:T(8,128)}) custom-call(f32[8,128,128]{2,1,0:T(8,128)S(1)} %get-tuple-element.6.ct_ref, f32[4,16,8,128]{3,2,1,0:T(8,128)S(1)} %get-tuple-element.7.wt_ref, s32[3,256]{1,0:T(4,128)S(1)} %copy-done.4, s32[3,512]{1,0:T(4,128)S(1)} %copy-done.2), custom_call_target="tpu_custom_call" | custom-call | tf_op jit(solution)/shard_map/combine/pallas_call | solution.py:434
Async XLA Ops:
  0.6 0.7 %copy-start.3 = (f32[2,4,128]{2,1,0:T(4,128)S(1)}, f32[2,4,128]{2,1,0:T(4,128)}, u32[]{:S(2)}) copy-start(f32[2,4,128]{2,1,0:T(4,128)} %vec_ref.1) | copy-start | bytes 12292
  1.3 0.9 %copy-start = (bf16[2,2,8,1,4096]{4,2,3,1,0:T(8,128)(2,1)S(1)}, bf16[2,2,8,1,4096]{4,2,3,1,0:T(8,128)(2,1)}, u32[]{:S(2)}) copy-start(bf16[2,2,8,1,4096]{4,2,3,1,0:T(8,128)(2,1)} %param.7) | copy-start | bytes 786436
  2.3 0.9 %copy-start.1 = (bf16[2,2,8,1,4096]{4,2,3,1,0:T(8,128)(2,1)S(1)}, bf16[2,2,8,1,4096]{4,2,3,1,0:T(8,128)(2,1)}, u32[]{:S(2)}) copy-start(bf16[2,2,8,1,4096]{4,2,3,1,0:T(8,128)(2,1)} %param.8) | copy-start | bytes 786436
  3.2 38.6 %copy-start.2 = (s32[3,512]{1,0:T(4,128)S(1)}, s32[3,512]{1,0:T(4,128)}, u32[]{:S(2)}) copy-start(s32[3,512]{1,0:T(4,128)} %cell_ref.1) | copy-start | bytes 18436
  3.2 38.6 %copy-start.4 = (s32[3,256]{1,0:T(4,128)S(1)}, s32[3,256]{1,0:T(4,128)}, u32[]{:S(2)}) copy-start(s32[3,256]{1,0:T(4,128)} %kpt_ref.1) | copy-start | bytes 9220

commit v2 on v0

v2 whole, which is shorter than its diff:
```python
import contextlib
import functools

import jax
import jax.numpy as jnp
import numpy as np
from jax import lax
from jax.experimental import pallas as pl
from jax.experimental.pallas import tpu as pltpu
from jax.sharding import PartitionSpec as P

MESH = pl.DeviceIdType.MESH
RING = (8, 4, 4)
NV = 8
NC = 8
LANES = 128
PTS = 32
GRANT = 67043328


def stage(name):
    return contextlib.nullcontext()


def drain(sem, ref):
    pltpu.make_async_copy(ref, ref, sem).wait()


COS30 = float(np.float32(jnp.bfloat16(np.cos(np.pi / 6))))
FIT = np.linalg.solve(
    np.array([[1.0, 1.0, 1.0], [1.0, 4.0, 16.0], [1.0, 9.0, 81.0]]),
    np.array([0.5, COS30 / 2, 1.0 / 3]),
)


def cosine(level):
    u = jnp.abs(level - 6.0) - 3.0
    square = u * u
    return u * (float(FIT[0]) + square * (float(FIT[1]) + square * float(FIT[2])))


def phases(kpt_ref, cell_ref, table):
    bf16, f32 = jnp.bfloat16, jnp.float32
    kpt = kpt_ref[...].astype(f32)
    cell = cell_ref[...].astype(f32)
    kpt = jnp.concatenate([kpt, jnp.zeros((5, kpt.shape[1]), f32)], 0).astype(bf16)
    cell = jnp.concatenate([cell, jnp.zeros((5, cell.shape[1]), f32)], 0).astype(bf16)
    rows = lax.broadcasted_iota(jnp.int32, (256, 256), 0)
    columns = lax.broadcasted_iota(jnp.int32, (256, 256), 1)
    source = 2 * jnp.bitwise_and(columns, 127) + jnp.right_shift(columns, 7)
    swap = jnp.where(rows == source, 1.0, 0.0).astype(bf16)
    kpt = jnp.dot(kpt, swap, preferred_element_type=f32)
    for a in range(2):
        part = jnp.transpose(kpt[:, a * 128 : a * 128 + 128]).astype(bf16)
        turns = jnp.dot(part, cell, preferred_element_type=f32)
        turns = turns - 12.0 * jnp.floor((turns + 0.5) * (1.0 / 12.0))
        cos = cosine(turns).astype(bf16)
        shifted = turns - 3.0
        sin = cosine(jnp.where(shifted < 0.0, shifted + 12.0, shifted)).astype(bf16)
        table[a * 256 : a * 256 + 128, 0:512] = cos
        table[a * 256 : a * 256 + 128, 512:1024] = sin
        table[a * 256 + 128 : a * 256 + 256, 0:512] = -sin
        table[a * 256 + 128 : a * 256 + 256, 512:1024] = cos


def exchange(
    ring,
    groups,
    nc,
    hole_hbm,
    vec_hbm,
    cond_hbm,
    val_hbm,
    kpt_hbm,
    cell_hbm,
    real_hbm,
    imag_hbm,
    hole_v,
    vec_v,
    kpt_v,
    cell_v,
    cond_v,
    val_v,
    dest,
    cx,
    cy,
    cf,
    cs,
    ct,
    vf,
    hi,
    hf,
    hs,
    wf,
    wt,
    table,
    lhs,
    real_v,
    imag_v,
    load_sem,
    out_sem,
    cx_send,
    cx_recv,
    cy_send,
    cy_recv,
    cz_send,
    cz_recv,
    vy_send,
    vy_recv,
    vz_send,
    vz_recv,
    vx_send,
    vx_recv,
    hi_send,
    hi_recv,
    hy_send,
    hy_recv,
    hz_send,
    hz_recv,
    hx_send,
    hx_recv,
    w_send,
    w_recv,
):
    ny, nx, nz = ring
    count = ny * nx * nz
    me = lax.axis_index("kgrp")
    img = lax.axis_index("img")
    y = lax.div(me, nx * nz)
    x = lax.rem(lax.div(me, nz), nx)
    z = lax.rem(me, nz)
    bf16, f32 = jnp.bfloat16, jnp.float32

    def at(yy, xx, zz, gg):
        return ((yy * nx + xx) * nz + zz, gg)

    def y_peer(step):
        yy = lax.rem(y + step, ny)
        return yy, at(yy, x, z, img)

    def x_peer(step):
        xx = lax.rem(x + step, nx)
        return xx, at(y, xx, z, img)

    def z_peer(step):
        zz = lax.rem(z + step, nz)
        return zz, at(y, x, zz, img)

    def img_peer(step):
        return (me, jnp.bitwise_xor(img, step))

    def send(src, dst, send_sem, recv_sem, device):
        pltpu.make_async_remote_copy(
            src_ref=src,
            dst_ref=dst,
            send_sem=send_sem,
            recv_sem=recv_sem,
            device_id=device,
            device_id_type=MESH,
        ).start()

    far_y = sorted(range(1, ny), key=lambda s: -min(s, ny - s))
    far_z = sorted(range(1, nz), key=lambda s: -min(s, nz - s))
    far_x = sorted(range(1, nx), key=lambda s: -min(s, nx - s))
    far_g = list(range(groups - 1, 0, -1))
    order = far_z + [0]

    barrier = pltpu.get_barrier_semaphore()
    peers = (
        [y_peer(s)[1] for s in far_y]
        + [z_peer(s)[1] for s in far_z]
        + [x_peer(s)[1] for s in far_x]
        + [img_peer(s) for s in far_g]
    )
    load_vec = pltpu.make_async_copy(vec_hbm, vec_v, load_sem.at[2])
    load_hole = pltpu.make_async_copy(hole_hbm, hole_v, load_sem.at[3])
    load_val = pltpu.make_async_copy(val_hbm, val_v, load_sem.at[0])
    load_cond = pltpu.make_async_copy(cond_hbm, cond_v, load_sem.at[1])
    load_kpt = pltpu.make_async_copy(kpt_hbm, kpt_v, load_sem.at[4])
    load_cell = pltpu.make_async_copy(cell_hbm, cell_v, load_sem.at[5])
    for load in (load_vec, load_hole, load_val, load_cond, load_kpt, load_cell):
        load.start()
    with stage("signal"):
        for peer in peers:
            pl.semaphore_signal(barrier, inc=1, device_id=peer, device_id_type=MESH)

    with stage("pack"):
        load_vec.wait()
        vf[y, x, z] = vec_v[...].reshape(8, vec_v.shape[2]).astype(vf.dtype)

    with stage("pick"):
        points = val_v.shape[1]
        load_hole.wait()
        wanted = hole_v[...] - img * points
        lane8 = lax.broadcasted_iota(jnp.int32, (8, LANES), 1)
        lane32 = lax.broadcasted_iota(jnp.int32, (32, LANES), 1)
        load_val.wait()

        def pick(j, kept):
            tile = val_v[:, pl.ds(pl.multiple_of(j * LANES, LANES), LANES)]
            return kept + jnp.where(lane32 + j * LANES == wanted, tile.astype(f32), 0.0)

        tile = lax.fori_loop(
            0, points // LANES, pick, jnp.zeros((32, LANES), f32), unroll=8
        )
        tile = jnp.concatenate([tile, jnp.zeros((LANES - 32, LANES), f32)], 0)
        tile = tile.astype(bf16)
        chosen = jnp.ones((8, LANES), bf16)
        row = lax.dot_general(
            chosen, tile, (((1,), (1,)), ((), ())), preferred_element_type=f32
        )
        hi[img] = row[0:1]

    low = lane8 < 64
    odd = lax.rem(lax.div(lane8, 32), 2) == 1

    def relay(j, carry):
        yy = lax.div(j, nx)
        xx = lax.rem(j, nx)
        column = pl.ds(pl.multiple_of(j * LANES, LANES), LANES)
        t = [cond_v[q, :, column].astype(f32) for q in range(4)]
        halves = []
        for q in range(2):
            halves.append(jnp.where(low, t[q], pltpu.roll(t[q + 2], 64, 1)))
        for q in range(2):
            halves.append(jnp.where(low, pltpu.roll(t[q], 64, 1), t[q + 2]))
        for h in range(2):
            first, second = halves[2 * h], halves[2 * h + 1]
            dest[yy, xx, 2 * h] = jnp.where(odd, pltpu.roll(second, 32, 1), first).astype(bf16)
            dest[yy, xx, 2 * h + 1] = jnp.where(odd, second, pltpu.roll(first, 96, 1)).astype(bf16)
        return carry

    with stage("relay"):
        load_cond.wait()
        lax.fori_loop(0, ny * nx, relay, 0, unroll=16)
        for zz in range(nz):
            for yy in range(ny):
                cx[zz, x, yy] = dest[yy, x, zz]

    with stage("barrier"):
        pl.semaphore_wait(barrier, len(peers))

    for s in far_y:
        send(vf.at[y, x, z], vf.at[y, x, z], vy_send, vy_recv, y_peer(s)[1])
    for s in far_g:
        send(hi.at[img], hi.at[img], hi_send, hi_recv, img_peer(s))
    for s in order:
        zz = lax.rem(z + s, nz)
        for t in far_x:
            xx, device = x_peer(t)
            send(dest.at[:, xx, zz], cx.at[zz, x], cx_send, cx_recv.at[s], device)

    with stage("phases"):
        load_kpt.wait()
        load_cell.wait()
        if count == LANES:
            phases(kpt_v, cell_v, table)

    with stage("hole_img"):
        drain(hi_recv, hi.at[pl.ds(0, groups - 1)])
    total = hi[0]
    for s in range(1, groups):
        total = total + hi[s]
    hf[y, x, z] = total

    def wait_x(s):
        zz = lax.rem(z + s, nz)
        with stage(f"cx{s}"):
            drain(cx_recv.at[s], cx.at[zz, pl.ds(0, nx - 1)])

    def forward_y(s):
        zz = lax.rem(z + s, nz)
        for t in far_y:
            yy, device = y_peer(t)
            send(cx.at[zz, :, yy], cy.at[zz, y], cy_send, cy_recv.at[s], device)
        for xx in range(nx):
            cy[zz, y, xx] = cx[zz, xx, y]

    wait_x(order[0])
    for s in far_y:
        send(hf.at[y, x, z], hf.at[y, x, z], hy_send, hy_recv, y_peer(s)[1])
    forward_y(order[0])
    for s in order[1:]:
        wait_x(s)
        forward_y(s)

    with stage("vec_y"):
        drain(vy_recv, vf.at[pl.ds(0, ny - 1), 0, 0])
    for t in far_z:
        send(vf.at[:, x, z], vf.at[:, x, z], vz_send, vz_recv.at[t], z_peer(t)[1])
    for t in far_x:
        send(vf.at[:, x, z], vf.at[:, x, z], vx_send, vx_recv, x_peer(t)[1])

    with stage("hole_y"):
        drain(hy_recv, hf.at[pl.ds(0, ny - 1), 0, 0])
    for t in far_z:
        send(hf.at[:, x, z], hf.at[:, x, z], hz_send, hz_recv, z_peer(t)[1])

    def forward_v(t):
        zz = lax.rem(z + nz - t, nz)
        with stage(f"vec_z{t}"):
            drain(vz_recv.at[t], vf.at[:, 0, 0])
        for u in far_x:
            send(vf.at[:, x, zz], vf.at[:, x, zz], vx_send, vx_recv, x_peer(u)[1])

    def forward_z(s):
        zz, device = z_peer(s)
        with stage(f"cy{s}"):
            drain(cy_recv.at[s], cy.at[zz, pl.ds(0, ny - 1)])
        send(cy.at[zz], cf.at[:, :, z], cz_send, cz_recv, device)

    near_z = far_z[::-1]
    for t in near_z[:-1]:
        forward_v(t)
    for s in far_z[:2]:
        forward_z(s)
    forward_v(near_z[-1])
    for s in far_z[2:]:
        forward_z(s)

    with stage("hole_z"):
        drain(hz_recv, hf.at[:, 0, pl.ds(0, nz - 1)])
    for t in far_x:
        send(hf.at[:, x], hf.at[:, x], hx_send, hx_recv, x_peer(t)[1])

    with stage("cy0"):
        drain(cy_recv.at[0], cy.at[z, pl.ds(0, ny - 1)])
        for yy in range(ny):
            for xx in range(nx):
                cf[yy, xx, z] = cy[z, yy, xx]

    with stage("vec_x"):
        drain(vx_recv, vf.at[:, pl.ds(0, nx - 1)])
    with stage("hole_x"):
        drain(hx_recv, hf.at[:, pl.ds(0, nx - 1)])

    with stage("weights"):
        for d in range(count):
            hs[pl.ds(d, 1), :] = hf[d // (nx * nz), d // nz % nx, d % nz]
        holes = jnp.transpose(hs[...])
        upper = lax.broadcasted_iota(jnp.int32, (8, vf.shape[4]), 0) < 4
        for a in range(2):
            for c in range(nc):
                along = None
                across = None
                for v in range(NV):
                    d = (a * NV + v) * nc + c
                    piece = vf[d // (nx * nz), d // nz % nx, d % nz].astype(f32)
                    real = piece * holes[a * 16 + v : a * 16 + v + 1]
                    imag = piece * holes[a * 16 + 8 + v : a * 16 + 9 + v]
                    along = real if along is None else along + real
                    across = imag if across is None else across + imag
                across = pltpu.roll(across, 4, 0)
                weight = (along + jnp.where(upper, across, -across)) * ((NV * NC) ** -0.5)
                wf[img, a * nc + c] = weight.astype(bf16)

    with stage("cz"):
        drain(cz_recv, cf.at[:, :, pl.ds(0, nz - 1)])
    for s in far_g:
        send(wf.at[img], wf.at[img], w_send, w_recv.at[s], img_peer(s))
    with stage("turn"):
        cs[...] = cf[...].astype(f32).reshape(cs.shape)
        for c in range(8):
            ct[c] = jnp.transpose(cs[pl.ds(c, count, 8), :])

    def products(step):
        group = jnp.bitwise_xor(img, step)
        wt[...] = wf[group].astype(f32)
        for a in range(2):
            for half in range(2):
                reals = []
                imags = []
                for c in range(nc):
                    start = a * 64 + half * 16
                    reals.append(ct[c, start : start + 16, :])
                    imags.append(ct[c, start + 32 : start + 48, :])
                for s in range(4):
                    out_real = None
                    out_imag = None
                    for c in range(nc):
                        wr = wt[a * nc + c, s : s + 1, :]
                        wi = wt[a * nc + c, s + 4 : s + 5, :]
                        tr = wr * reals[c] - wi * imags[c]
                        ti = wr * imags[c] + wi * reals[c]
                        out_real = tr if out_real is None else out_real + tr
                        out_imag = ti if out_imag is None else out_imag + ti
                    first = step * 128 + s * 32 + half * 16
                    left = a * 2 * count
                    lhs[first : first + 16, left : left + count] = out_real.astype(bf16)
                    lhs[first : first + 16, left + count : left + 2 * count] = out_imag.astype(bf16)

    def finish(first, last):
        rows = slice(first * 128, last * 128)
        outs = []
        for part, (held, out) in enumerate(((real_v, real_hbm), (imag_v, imag_hbm))):
            held[rows, :] = jnp.dot(
                lhs[rows, :],
                table[0 : 4 * count, part * 512 : part * 512 + 512],
                preferred_element_type=f32,
            ) * (512.0**-0.5)
            for step in range(first, last):
                group = jnp.bitwise_xor(img, step)
                outs.append(
                    pltpu.make_async_copy(
                        held.at[pl.ds(step * 128, 128)],
                        out.at[pl.ds(pl.multiple_of(group * 128, 128), 128)],
                        out_sem.at[part, step],
                    )
                )
                outs[-1].start()
        return outs

    with stage("own"):
        products(0)
        outs = finish(0, 1)
    for s in far_g[::-1]:
        with stage(f"wimg{s}"):
            drain(w_recv.at[s], wf.at[0])
        with stage("products"):
            products(s)
    with stage("finish"):
        outs = outs + finish(1, groups)

    with stage("sends"):
        drain(hi_send, hi.at[pl.ds(0, groups - 1)])
        drain(vy_send, vf.at[pl.ds(0, ny - 1), 0, 0])
        drain(vz_send, vf.at[:, 0, pl.ds(0, nz - 1)])
        drain(vx_send, vf.at[:, pl.ds(0, nx - 1)])
        drain(hy_send, hf.at[pl.ds(0, ny - 1), 0, 0])
        drain(hz_send, hf.at[:, 0, pl.ds(0, nz - 1)])
        drain(hx_send, hf.at[:, pl.ds(0, nx - 1)])
        drain(cx_send, cx.at[:, pl.ds(0, nx - 1)])
        drain(cy_send, cy.at[:, pl.ds(0, ny - 1)])
        drain(cz_send, cf.at[:, :, pl.ds(0, nz - 1)])
        drain(w_send, wf.at[pl.ds(0, groups - 1)])
    with stage("outs"):
        for out in outs:
            out.wait()


def run_exchange(ring, groups, nc, hole, vec, cond, val, kpt, cell, vec_type=jnp.bfloat16):
    ny, nx, nz = ring
    count = ny * nx * nz
    lanes = vec.shape[2]
    bf16, f32, i32 = jnp.bfloat16, jnp.float32, jnp.int32
    dma = pltpu.SemaphoreType.DMA
    rows = groups * 4 * PTS
    anywhere = pl.BlockSpec(memory_space=pltpu.HBM)
    scratch = [
        pltpu.VMEM(hole.shape, i32),
        pltpu.VMEM(vec.shape, f32),
        pltpu.VMEM(kpt.shape, i32),
        pltpu.VMEM(cell.shape, i32),
        pltpu.VMEM(cond.shape, bf16),
        pltpu.VMEM(val.shape, bf16),
        pltpu.VMEM((ny, nx, nz, 8, LANES), bf16),
        pltpu.VMEM((nz, nx, ny, 8, LANES), bf16),
        pltpu.VMEM((nz, ny, nx, 8, LANES), bf16),
        pltpu.VMEM((ny, nx, nz, 8, LANES), bf16),
        pltpu.VMEM((count * 8, LANES), f32),
        pltpu.VMEM((8, LANES, count), f32),
        pltpu.VMEM((ny, nx, nz, 8, lanes), vec_type),
        pltpu.VMEM((groups, 1, LANES), f32),
        pltpu.VMEM((ny, nx, nz, 1, LANES), f32),
        pltpu.VMEM((count, LANES), f32),
        pltpu.VMEM((groups, 2 * nc, 8, lanes), bf16),
        pltpu.VMEM((2 * nc, 8, lanes), f32),
        pltpu.VMEM((512, 1024), bf16),
        pltpu.VMEM((rows, 4 * count), bf16),
        pltpu.VMEM((rows, 512), f32),
        pltpu.VMEM((rows, 512), f32),
        dma((6,)),
        dma((2, groups)),
        dma(()),
        dma((nz,)),
        dma(()),
        dma((nz,)),
        dma(()),
        dma(()),
        dma(()),
        dma(()),
        dma(()),
        dma((nz,)),
        dma(()),
        dma(()),
        dma(()),
        dma(()),
        dma(()),
        dma(()),
        dma(()),
        dma(()),
        dma(()),
        dma(()),
        dma(()),
        dma((groups,)),
    ]
    return pl.pallas_call(
        functools.partial(exchange, ring, groups, nc),
        out_shape=(
            jax.ShapeDtypeStruct((rows, 512), f32),
            jax.ShapeDtypeStruct((rows, 512), f32),
        ),
        in_specs=[anywhere] * 6,
        out_specs=(anywhere, anywhere),
        scratch_shapes=scratch,
        compiler_params=pltpu.CompilerParams(
            collective_id=0, has_side_effects=True, vmem_limit_bytes=GRANT
        ),
        name="exchange",
    )(hole, vec, cond, val, kpt, cell)


def shards(vectors, conduction, valence, hole_point, kpoint_grid, image_cells):
    points = conduction.shape[4]
    cond = conduction.reshape(4, 8, points)
    val = valence.reshape(32, points)
    real, imag = run_exchange(
        RING,
        lax.axis_size("img"),
        NC,
        hole_point.reshape(1, 1),
        vectors,
        cond,
        val,
        kpoint_grid,
        image_cells,
    )
    shape = (16, 1, PTS, 512)
    return real.reshape(shape), imag.reshape(shape)


def solution(mesh):
    placed = (
        P(None, "img", "kgrp"),
        P("kgrp", None, None, "img", None),
        P("kgrp", None, None, "img", None),
        P(),
        P(),
        P(),
    )
    return jax.shard_map(
        shards,
        mesh=mesh,
        in_specs=placed,
        out_specs=(P(None, "img", "kgrp", None), P(None, "img", "kgrp", None)),
        check_vma=False,
    )
```

time: 112 us -> 41 us (0.37)
  Pallas kernels: 0 us -> 36.2 us
  local copies, waits for them, and re-layouts: 36.4 us -> 3.35 us
  starting transfers between devices: 29.6 us -> 0 us
  waiting for transfers between devices: 26.2 us -> 0 us
  blocking collectives: 13.7 us -> 0 us
  matrix products: 2.29 us -> 0 us
  other arithmetic: 2.02 us -> 0 us
    pallas_call x0 -> x1, Pallas kernels: none -> 36.2 us  [run_exchange(): pl.pallas_call(functools.partial(exchange, ring, groups, nc), out_shape=(...]
    all_to_all x2 -> x0, starting transfers between devices: 29.6 us -> none  [the longest x1 20.8 us: shards(): lax.all_to_all(columns, 'kgrp', split_axis=2, concat_axis=2, tiled=True)]
    all_to_all x2 -> x0, waiting for transfers between devices: 26.2 us -> none  [the longest x1 20 us: shards(): lax.all_to_all(products, 'kgrp', split_axis=3, concat_axis=2, tiled=True)]
    unnamed x10 -> x4, local copies, waits for them, and re-layouts: 20.1 us -> 3.35 us
    all_to_all x1 -> x0, local copies, waits for them, and re-layouts: 8.56 us -> none  [shards(): lax.all_to_all(products, 'kgrp', split_axis=3, concat_axis=2, tiled=True)]
    all_gather x1 -> x0, blocking collectives: 7.73 us -> none  [shards(): all_columns = lax.all_gather(owned_columns, 'img', axis=1, tiled=True)]
    convert_element_type x1 -> x0, local copies, waits for them, and re-layouts: 7.13 us -> none  [shards(): products = jnp.einsum('kasbc,kbcp->sakp', mixing(weights), conduction[:,...]
    psum x1 -> x0, blocking collectives: 5.97 us -> none  [shards(): hole_values = lax.psum(picked, 'img')]
  transfers between devices with their start and end apart: 2 -> 0, of which waited for: 2 -> 0; matrix products, arithmetic and copies ran while one was open for 2% -> 0% of each run, Pallas kernels for 0% -> 0%
where the time goes in v2:
time: 41 us; the launch traced here: 40.8 us
  Pallas kernels  36.2 us (88%)
  local copies, waits for them, and re-layouts  3.35 us (8%)
  between operations  1.29 us (3%)
    pallas_call x1, Pallas kernels, run_exchange(): pl.pallas_call(functools.partial(exchange, ring, groups, nc), out_shape=(...  36.2 us
    unnamed x4, local copies, waits for them, and re-layouts  3.35 us

profile of v2, /device:TPU:1, one launch (start us, length us, event | category | flops | bytes accessed | tf_op | source)
XLA Modules:
  0.0 40.8 jit_solution(12040344037404217314)
XLA Ops:
  1.3 36.2 %exchange.1 = (f32[512,512]{1,0:T(8,128)}, f32[512,512]{1,0:T(8,128)}) custom-call(s32[1,1]{1,0:T(1,128)} %bitcast.9.hole_hbm, f32[2,4,128]{2,1,0:T(4,128)} %vec_hbm.1, bf16[4,8,4096]{2,1,0:T(8,128)(2,1)} %bitcast.12, bf16[32,4096]{1,0:T(8,128)(2,1)} %bitcast.13, s32[3,256]{1,0:T(4,128)} %kpt_hbm.1, s32[3,512]{1,0:T(4,128)} %cell_hbm.1), custom_call_target="tpu_custom_call" | custom-call | tf_op jit(solution)/shard_map/exchange/pallas_call | solution.py:497
  37.5 0.0 copy-start
  37.5 2.4 %copy.13 = f32[16,1,32,512]{3,2,1,0:T(8,128)} copy(f32[16,1,32,512]{3,2,1,0:T(8,128)} %bitcast.11) | data formatting | bytes 2097152
  39.9 0.0 copy-done
  39.9 1.0 %copy.14 = f32[16,1,32,512]{3,2,1,0:T(8,128)} copy(f32[16,1,32,512]{3,2,1,0:T(8,128)S(1)} %bitcast.10) | data formatting | bytes 2097152
Async XLA Ops:
  37.5 2.4 %copy-start = (f32[512,512]{1,0:T(8,128)S(1)}, f32[512,512]{1,0:T(8,128)}, u32[]{:S(2)}) copy-start(f32[512,512]{1,0:T(8,128)} %get-tuple-element.5) | copy-start | bytes 3145732

commit v3 on v2

--- a/solution.py
+++ b/solution.py
@@ -15,7 +15,7 @@
 NC = 8
 LANES = 128
 PTS = 32
-GRANT = 67043328
+GRANT = 24 * 1024 * 1024
 
 
 def stage(name):
@@ -73,8 +73,8 @@
     val_hbm,
     kpt_hbm,
     cell_hbm,
-    real_hbm,
-    imag_hbm,
+    lhs,
+    table,
     hole_v,
     vec_v,
     kpt_v,
@@ -88,17 +88,14 @@
     cs,
     ct,
     vf,
-    hi,
-    hf,
+    hy,
+    hz,
+    hq,
+    hw,
     hs,
     wf,
     wt,
-    table,
-    lhs,
-    real_v,
-    imag_v,
     load_sem,
-    out_sem,
     cx_send,
     cx_recv,
     cy_send,
@@ -111,8 +108,6 @@
     vz_recv,
     vx_send,
     vx_recv,
-    hi_send,
-    hi_recv,
     hy_send,
     hy_recv,
     hz_send,
@@ -149,6 +144,9 @@
     def img_peer(step):
         return (me, jnp.bitwise_xor(img, step))
 
+    def corner(step, flip):
+        return at(y, lax.rem(x + step, nx), z, jnp.bitwise_xor(img, flip))
+
     def send(src, dst, send_sem, recv_sem, device):
         pltpu.make_async_remote_copy(
             src_ref=src,
@@ -171,7 +169,11 @@
         + [z_peer(s)[1] for s in far_z]
         + [x_peer(s)[1] for s in far_x]
         + [img_peer(s) for s in far_g]
+        + [corner(s, t) for s in far_x for t in far_g]
     )
+    with stage("signal"):
+        for peer in peers:
+            pl.semaphore_signal(barrier, inc=1, device_id=peer, device_id_type=MESH)
     load_vec = pltpu.make_async_copy(vec_hbm, vec_v, load_sem.at[2])
     load_hole = pltpu.make_async_copy(hole_hbm, hole_v, load_sem.at[3])
     load_val = pltpu.make_async_copy(val_hbm, val_v, load_sem.at[0])
@@ -180,9 +182,6 @@
     load_cell = pltpu.make_async_copy(cell_hbm, cell_v, load_sem.at[5])
     for load in (load_vec, load_hole, load_val, load_cond, load_kpt, load_cell):
         load.start()
-    with stage("signal"):
-        for peer in peers:
-            pl.semaphore_signal(barrier, inc=1, device_id=peer, device_id_type=MESH)
 
     with stage("pack"):
         load_vec.wait()
@@ -204,12 +203,12 @@
             0, points // LANES, pick, jnp.zeros((32, LANES), f32), unroll=8
         )
         tile = jnp.concatenate([tile, jnp.zeros((LANES - 32, LANES), f32)], 0)
-        tile = tile.astype(bf16)
+        tile = pltpu.roll(tile, z * 32, 0).astype(bf16)
         chosen = jnp.ones((8, LANES), bf16)
         row = lax.dot_general(
             chosen, tile, (((1,), (1,)), ((), ())), preferred_element_type=f32
         )
-        hi[img] = row[0:1]
+        hy[y] = row[0:1]
 
     low = lane8 < 64
     odd = lax.rem(lax.div(lane8, 32), 2) == 1
@@ -242,8 +241,8 @@
 
     for s in far_y:
         send(vf.at[y, x, z], vf.at[y, x, z], vy_send, vy_recv, y_peer(s)[1])
-    for s in far_g:
-        send(hi.at[img], hi.at[img], hi_send, hi_recv, img_peer(s))
+    for s in far_y:
+        send(hy.at[y], hy.at[y], hy_send, hy_recv, y_peer(s)[1])
     for s in order:
         zz = lax.rem(z + s, nz)
         for t in far_x:
@@ -255,13 +254,6 @@
         load_cell.wait()
         if count == LANES:
             phases(kpt_v, cell_v, table)
-
-    with stage("hole_img"):
-        drain(hi_recv, hi.at[pl.ds(0, groups - 1)])
-    total = hi[0]
-    for s in range(1, groups):
-        total = total + hi[s]
-    hf[y, x, z] = total
 
     def wait_x(s):
         zz = lax.rem(z + s, nz)
@@ -276,11 +268,7 @@
         for xx in range(nx):
             cy[zz, y, xx] = cx[zz, xx, y]
 
-    wait_x(order[0])
-    for s in far_y:
-        send(hf.at[y, x, z], hf.at[y, x, z], hy_send, hy_recv, y_peer(s)[1])
-    forward_y(order[0])
-    for s in order[1:]:
+    for s in order:
         wait_x(s)
         forward_y(s)
 
@@ -292,9 +280,10 @@
         send(vf.at[:, x, z], vf.at[:, x, z], vx_send, vx_recv, x_peer(t)[1])
 
     with stage("hole_y"):
-        drain(hy_recv, hf.at[pl.ds(0, ny - 1), 0, 0])
+        drain(hy_recv, hy.at[pl.ds(0, ny - 1)])
     for t in far_z:
-        send(hf.at[:, x, z], hf.at[:, x, z], hz_send, hz_recv, z_peer(t)[1])
+        send(hy, hz.at[z], hz_send, hz_recv, z_peer(t)[1])
+    hz[z] = hy[...]
 
     def forward_v(t):
         zz = lax.rem(z + nz - t, nz)
@@ -315,13 +304,24 @@
     for s in far_z[:2]:
         forward_z(s)
     forward_v(near_z[-1])
+
+    with stage("hole_z"):
+        drain(hz_recv, hz.at[pl.ds(0, nz - 1)])
+        packed = hz[0]
+        for t in range(1, nz):
+            packed = packed + hz[t]
+        hq[x, img] = packed
     for s in far_z[2:]:
         forward_z(s)
-
-    with stage("hole_z"):
-        drain(hz_recv, hf.at[:, 0, pl.ds(0, nz - 1)])
-    for t in far_x:
-        send(hf.at[:, x], hf.at[:, x], hx_send, hx_recv, x_peer(t)[1])
+    for s in far_x:
+        send(hq.at[x, img], hq.at[x, img], hx_send, hx_recv, x_peer(s)[1])
+        for t in far_g:
+            send(hq.at[x, img], hq.at[x, img], hx_send, hx_recv, corner(s, t))
+    for t in far_g:
+        send(hq.at[x, img], hq.at[x, img], hx_send, hx_recv, img_peer(t))
+
+    def wait_holes(sem):
+        pltpu.make_async_copy(hw, hw, sem).wait()
 
     with stage("cy0"):
         drain(cy_recv.at[0], cy.at[z, pl.ds(0, ny - 1)])
@@ -332,11 +332,17 @@
     with stage("vec_x"):
         drain(vx_recv, vf.at[:, pl.ds(0, nx - 1)])
     with stage("hole_x"):
-        drain(hx_recv, hf.at[:, pl.ds(0, nx - 1)])
+        wait_holes(hx_recv)
 
     with stage("weights"):
-        for d in range(count):
-            hs[pl.ds(d, 1), :] = hf[d // (nx * nz), d // nz % nx, d % nz]
+        for xx in range(nx):
+            part = hq[xx, 0]
+            for t in range(1, groups):
+                part = part + hq[xx, t]
+            part = part.reshape(ny, LANES)
+            for zz in range(nz):
+                turned = part if zz == 0 else pltpu.roll(part, LANES - 32 * zz, 1)
+                hs[pl.ds(xx * nz + zz, ny, nx * nz), :] = turned
         holes = jnp.transpose(hs[...])
         upper = lax.broadcasted_iota(jnp.int32, (8, vf.shape[4]), 0) < 4
         for a in range(2):
@@ -354,10 +360,10 @@
                 weight = (along + jnp.where(upper, across, -across)) * ((NV * NC) ** -0.5)
                 wf[img, a * nc + c] = weight.astype(bf16)
 
+    for s in far_g[::-1]:
+        send(wf.at[img], wf.at[img], w_send, w_recv.at[s], img_peer(s))
     with stage("cz"):
         drain(cz_recv, cf.at[:, :, pl.ds(0, nz - 1)])
-    for s in far_g:
-        send(wf.at[img], wf.at[img], w_send, w_recv.at[s], img_peer(s))
     with stage("turn"):
         cs[...] = cf[...].astype(f32).reshape(cs.shape)
         for c in range(8):
@@ -384,58 +390,31 @@
                         ti = wr * imags[c] + wi * reals[c]
                         out_real = tr if out_real is None else out_real + tr
                         out_imag = ti if out_imag is None else out_imag + ti
-                    first = step * 128 + s * 32 + half * 16
+                    first = pl.multiple_of(group * 128 + (s * 32 + half * 16), 16)
                     left = a * 2 * count
-                    lhs[first : first + 16, left : left + count] = out_real.astype(bf16)
-                    lhs[first : first + 16, left + count : left + 2 * count] = out_imag.astype(bf16)
-
-    def finish(first, last):
-        rows = slice(first * 128, last * 128)
-        outs = []
-        for part, (held, out) in enumerate(((real_v, real_hbm), (imag_v, imag_hbm))):
-            held[rows, :] = jnp.dot(
-                lhs[rows, :],
-                table[0 : 4 * count, part * 512 : part * 512 + 512],
-                preferred_element_type=f32,
-            ) * (512.0**-0.5)
-            for step in range(first, last):
-                group = jnp.bitwise_xor(img, step)
-                outs.append(
-                    pltpu.make_async_copy(
-                        held.at[pl.ds(step * 128, 128)],
-                        out.at[pl.ds(pl.multiple_of(group * 128, 128), 128)],
-                        out_sem.at[part, step],
-                    )
-                )
-                outs[-1].start()
-        return outs
+                    here = pl.ds(first, 16)
+                    lhs[here, left : left + count] = out_real.astype(bf16)
+                    lhs[here, left + count : left + 2 * count] = out_imag.astype(bf16)
 
     with stage("own"):
         products(0)
-        outs = finish(0, 1)
     for s in far_g[::-1]:
         with stage(f"wimg{s}"):
             drain(w_recv.at[s], wf.at[0])
         with stage("products"):
             products(s)
-    with stage("finish"):
-        outs = outs + finish(1, groups)
 
     with stage("sends"):
-        drain(hi_send, hi.at[pl.ds(0, groups - 1)])
         drain(vy_send, vf.at[pl.ds(0, ny - 1), 0, 0])
         drain(vz_send, vf.at[:, 0, pl.ds(0, nz - 1)])
         drain(vx_send, vf.at[:, pl.ds(0, nx - 1)])
-        drain(hy_send, hf.at[pl.ds(0, ny - 1), 0, 0])
-        drain(hz_send, hf.at[:, 0, pl.ds(0, nz - 1)])
-        drain(hx_send, hf.at[:, pl.ds(0, nx - 1)])
+        drain(hy_send, hy.at[pl.ds(0, ny - 1)])
+        drain(hz_send, hz.at[pl.ds(0, nz - 1)])
+        wait_holes(hx_send)
         drain(cx_send, cx.at[:, pl.ds(0, nx - 1)])
         drain(cy_send, cy.at[:, pl.ds(0, ny - 1)])
         drain(cz_send, cf.at[:, :, pl.ds(0, nz - 1)])
         drain(w_send, wf.at[pl.ds(0, groups - 1)])
-    with stage("outs"):
-        for out in outs:
-            out.wait()
 
 
 def run_exchange(ring, groups, nc, hole, vec, cond, val, kpt, cell, vec_type=jnp.bfloat16):
@@ -446,6 +425,7 @@
     dma = pltpu.SemaphoreType.DMA
     rows = groups * 4 * PTS
     anywhere = pl.BlockSpec(memory_space=pltpu.HBM)
+    vmem = pl.BlockSpec(memory_space=pltpu.VMEM)
     scratch = [
         pltpu.VMEM(hole.shape, i32),
         pltpu.VMEM(vec.shape, f32),
@@ -460,17 +440,14 @@
         pltpu.VMEM((count * 8, LANES), f32),
         pltpu.VMEM((8, LANES, count), f32),
         pltpu.VMEM((ny, nx, nz, 8, lanes), vec_type),
-        pltpu.VMEM((groups, 1, LANES), f32),
-        pltpu.VMEM((ny, nx, nz, 1, LANES), f32),
+        pltpu.VMEM((ny, 1, LANES), f32),
+        pltpu.VMEM((nz, ny, 1, LANES), f32),
+        pltpu.VMEM((nx, groups, ny, 1, LANES), f32),
+        pltpu.VMEM((nx * groups - 1, ny, 1, LANES), f32),
         pltpu.VMEM((count, LANES), f32),
         pltpu.VMEM((groups, 2 * nc, 8, lanes), bf16),
         pltpu.VMEM((2 * nc, 8, lanes), f32),
-        pltpu.VMEM((512, 1024), bf16),
-        pltpu.VMEM((rows, 4 * count), bf16),
-        pltpu.VMEM((rows, 512), f32),
-        pltpu.VMEM((rows, 512), f32),
         dma((6,)),
-        dma((2, groups)),
         dma(()),
         dma((nz,)),
         dma(()),
@@ -481,8 +458,6 @@
         dma(()),
         dma(()),
         dma((nz,)),
-        dma(()),
-        dma(()),
         dma(()),
         dma(()),
         dma(()),
@@ -497,24 +472,53 @@
     return pl.pallas_call(
         functools.partial(exchange, ring, groups, nc),
         out_shape=(
-            jax.ShapeDtypeStruct((rows, 512), f32),
-            jax.ShapeDtypeStruct((rows, 512), f32),
+            jax.ShapeDtypeStruct((rows, 4 * count), bf16),
+            jax.ShapeDtypeStruct((512, 1024), bf16),
         ),
         in_specs=[anywhere] * 6,
-        out_specs=(anywhere, anywhere),
+        out_specs=(vmem, vmem),
         scratch_shapes=scratch,
         compiler_params=pltpu.CompilerParams(
             collective_id=0, has_side_effects=True, vmem_limit_bytes=GRANT
         ),
         name="exchange",
-    )(hole, vec, cond, val, kpt, cell)
+    )(hole, *(pltpu.with_memory_space_constraint(v, pltpu.HBM) for v in (vec, cond, val, kpt, cell)))
+
+
+def combine(lhs, table, real_ref, imag_ref):
+    half = real_ref.shape[1]
+    scale = 512.0**-0.5
+    for part, ref in ((0, real_ref), (1, imag_ref)):
+        start = pl.multiple_of(part * 512 + pl.program_id(0) * half, half)
+        ref[...] = (
+            jnp.dot(lhs[...], table[:, pl.ds(start, half)], preferred_element_type=jnp.float32)
+            * scale
+        )
+
+
+def run_combine(lhs, table):
+    rows = lhs.shape[0]
+    vmem = pl.BlockSpec(memory_space=pltpu.VMEM)
+    block = pl.BlockSpec((rows, 256), lambda i: (0, i))
+    return pl.pallas_call(
+        combine,
+        grid=(2,),
+        out_shape=(
+            jax.ShapeDtypeStruct((rows, 512), jnp.float32),
+            jax.ShapeDtypeStruct((rows, 512), jnp.float32),
+        ),
+        in_specs=[vmem, vmem],
+        out_specs=(block, block),
+        compiler_params=pltpu.CompilerParams(vmem_limit_bytes=GRANT),
+        name="combine",
+    )(lhs, table)
 
 
 def shards(vectors, conduction, valence, hole_point, kpoint_grid, image_cells):
     points = conduction.shape[4]
     cond = conduction.reshape(4, 8, points)
     val = valence.reshape(32, points)
-    real, imag = run_exchange(
+    lhs, table = run_exchange(
         RING,
         lax.axis_size("img"),
         NC,
@@ -525,6 +529,7 @@
         kpoint_grid,
         image_cells,
     )
+    real, imag = run_combine(lhs, table)
     shape = (16, 1, PTS, 512)
     return real.reshape(shape), imag.reshape(shape)
 

time: 41 us -> 39.5 us (0.963)
  local copies, waits for them, and re-layouts: 3.35 us -> 0 us
  Pallas kernels: 36.2 us -> 38.1 us
    unnamed x4 -> x0, local copies, waits for them, and re-layouts: 3.35 us -> none
    pallas_call x0 -> x1, Pallas kernels: none -> 1.9 us  [run_combine(): pl.pallas_call(combine, grid=(2,), out_shape=(jax.ShapeDtypeStruct((rows,...]
where the time goes in v3:
time: 39.5 us; the launch traced here: 39.4 us
  Pallas kernels  38.1 us (96%)
  between operations  1.28 us (3%)
    pallas_call x1, Pallas kernels, run_exchange(): pl.pallas_call(functools.partial(exchange, ring, groups, nc), out_shape=(...  36.2 us
    pallas_call x1, Pallas kernels, run_combine(): pl.pallas_call(combine, grid=(2,), out_shape=(jax.ShapeDtypeStruct((rows,...  1.9 us

profile of v3, /device:TPU:1, one launch (start us, length us, event | category | flops | bytes accessed | tf_op | source)
XLA Modules:
  0.0 39.4 jit_solution(15431220752951646460)
XLA Ops:
  1.3 36.2 %exchange.1 = (bf16[512,512]{1,0:T(8,128)(2,1)S(1)}, bf16[512,1024]{1,0:T(8,128)(2,1)S(1)}) custom-call(s32[1,1]{1,0:T(1,128)} %bitcast.9.hole_hbm, f32[2,4,128]{2,1,0:T(4,128)} %vec_hbm.1, bf16[4,8,4096]{2,1,0:T(8,128)(2,1)} %bitcast.10, bf16[32,4096]{1,0:T(8,128)(2,1)} %bitcast.11, s32[3,256]{1,0:T(4,128)} %kpt_hbm.1, s32[3,512]{1,0:T(4,128)} %cell_hbm.1), custom_call_target="tpu_custom_call" | custom-call | tf_op jit(solution)/shard_map/exchange/pallas_call | solution.py:472
  37.5 1.9 %combine.1 = (f32[512,512]{1,0:T(8,128)}, f32[512,512]{1,0:T(8,128)}) custom-call(bf16[512,512]{1,0:T(8,128)(2,1)S(1)} %get-tuple-element.6.lhs, bf16[512,1024]{1,0:T(8,128)(2,1)S(1)} %get-tuple-element.7.table), custom_call_target="tpu_custom_call" | custom-call | tf_op jit(solution)/shard_map/combine/pallas_call | solution.py:503

commit v4 on v3

--- a/solution.py
+++ b/solution.py
@@ -88,7 +88,7 @@
     cs,
     ct,
     vf,
-    hy,
+    hx,
     hz,
     hq,
     hw,
@@ -208,7 +208,7 @@
         row = lax.dot_general(
             chosen, tile, (((1,), (1,)), ((), ())), preferred_element_type=f32
         )
-        hy[y] = row[0:1]
+        hx[x, img] = row[0:1]
 
     low = lane8 < 64
     odd = lax.rem(lax.div(lane8, 32), 2) == 1
@@ -239,10 +239,15 @@
     with stage("barrier"):
         pl.semaphore_wait(barrier, len(peers))
 
+    mine = hx.at[x, img]
+    for s in far_x:
+        for t in far_g:
+            send(mine, mine, hx_send, hx_recv, corner(s, t))
+        send(mine, mine, hx_send, hx_recv, x_peer(s)[1])
+    for t in far_g:
+        send(mine, mine, hx_send, hx_recv, img_peer(t))
     for s in far_y:
         send(vf.at[y, x, z], vf.at[y, x, z], vy_send, vy_recv, y_peer(s)[1])
-    for s in far_y:
-        send(hy.at[y], hy.at[y], hy_send, hy_recv, y_peer(s)[1])
     for s in order:
         zz = lax.rem(z + s, nz)
         for t in far_x:
@@ -268,9 +273,22 @@
         for xx in range(nx):
             cy[zz, y, xx] = cx[zz, xx, y]
 
-    for s in order:
-        wait_x(s)
-        forward_y(s)
+    def wait_holes(sem):
+        pltpu.make_async_copy(hw, hw, sem).wait()
+
+    with stage("hole_x"):
+        wait_holes(hx_recv)
+        for xx in range(nx):
+            total = hx[xx, 0]
+            for t in range(1, groups):
+                total = total + hx[xx, t]
+            hz[z, xx] = total
+    wait_x(order[0])
+    forward_y(order[0])
+    for t in far_z:
+        send(hz.at[z], hz.at[z], hz_send, hz_recv, z_peer(t)[1])
+    wait_x(order[1])
+    forward_y(order[1])
 
     with stage("vec_y"):
         drain(vy_recv, vf.at[pl.ds(0, ny - 1), 0, 0])
@@ -278,12 +296,9 @@
         send(vf.at[:, x, z], vf.at[:, x, z], vz_send, vz_recv.at[t], z_peer(t)[1])
     for t in far_x:
         send(vf.at[:, x, z], vf.at[:, x, z], vx_send, vx_recv, x_peer(t)[1])
-
-    with stage("hole_y"):
-        drain(hy_recv, hy.at[pl.ds(0, ny - 1)])
-    for t in far_z:
-        send(hy, hz.at[z], hz_send, hz_recv, z_peer(t)[1])
-    hz[z] = hy[...]
+    for s in order[2:]:
+        wait_x(s)
+        forward_y(s)
 
     def forward_v(t):
         zz = lax.rem(z + nz - t, nz)
@@ -299,29 +314,20 @@
         send(cy.at[zz], cf.at[:, :, z], cz_send, cz_recv, device)
 
     near_z = far_z[::-1]
-    for t in near_z[:-1]:
-        forward_v(t)
-    for s in far_z[:2]:
-        forward_z(s)
-    forward_v(near_z[-1])
-
     with stage("hole_z"):
         drain(hz_recv, hz.at[pl.ds(0, nz - 1)])
         packed = hz[0]
         for t in range(1, nz):
             packed = packed + hz[t]
-        hq[x, img] = packed
-    for s in far_z[2:]:
+        hq[y] = packed
+    for t in near_z[:-1]:
+        forward_v(t)
+    for s in far_y:
+        send(hq.at[y], hq.at[y], hy_send, hy_recv, y_peer(s)[1])
+    forward_z(far_z[0])
+    forward_v(near_z[-1])
+    for s in far_z[1:]:
         forward_z(s)
-    for s in far_x:
-        send(hq.at[x, img], hq.at[x, img], hx_send, hx_recv, x_peer(s)[1])
-        for t in far_g:
-            send(hq.at[x, img], hq.at[x, img], hx_send, hx_recv, corner(s, t))
-    for t in far_g:
-        send(hq.at[x, img], hq.at[x, img], hx_send, hx_recv, img_peer(t))
-
-    def wait_holes(sem):
-        pltpu.make_async_copy(hw, hw, sem).wait()
 
     with stage("cy0"):
         drain(cy_recv.at[0], cy.at[z, pl.ds(0, ny - 1)])
@@ -331,18 +337,14 @@
 
     with stage("vec_x"):
         drain(vx_recv, vf.at[:, pl.ds(0, nx - 1)])
-    with stage("hole_x"):
-        wait_holes(hx_recv)
+    with stage("hole_y"):
+        drain(hy_recv, hq.at[pl.ds(0, ny - 1)])
 
     with stage("weights"):
-        for xx in range(nx):
-            part = hq[xx, 0]
-            for t in range(1, groups):
-                part = part + hq[xx, t]
-            part = part.reshape(ny, LANES)
-            for zz in range(nz):
-                turned = part if zz == 0 else pltpu.roll(part, LANES - 32 * zz, 1)
-                hs[pl.ds(xx * nz + zz, ny, nx * nz), :] = turned
+        part = hq[...].reshape(ny * nx, LANES)
+        for zz in range(nz):
+            turned = part if zz == 0 else pltpu.roll(part, LANES - 32 * zz, 1)
+            hs[pl.ds(zz, ny * nx, nz), :] = turned
         holes = jnp.transpose(hs[...])
         upper = lax.broadcasted_iota(jnp.int32, (8, vf.shape[4]), 0) < 4
         for a in range(2):
@@ -408,7 +410,7 @@
         drain(vy_send, vf.at[pl.ds(0, ny - 1), 0, 0])
         drain(vz_send, vf.at[:, 0, pl.ds(0, nz - 1)])
         drain(vx_send, vf.at[:, pl.ds(0, nx - 1)])
-        drain(hy_send, hy.at[pl.ds(0, ny - 1)])
+        drain(hy_send, hq.at[pl.ds(0, ny - 1)])
         drain(hz_send, hz.at[pl.ds(0, nz - 1)])
         wait_holes(hx_send)
         drain(cx_send, cx.at[:, pl.ds(0, nx - 1)])
@@ -440,10 +442,10 @@
         pltpu.VMEM((count * 8, LANES), f32),
         pltpu.VMEM((8, LANES, count), f32),
         pltpu.VMEM((ny, nx, nz, 8, lanes), vec_type),
-        pltpu.VMEM((ny, 1, LANES), f32),
-        pltpu.VMEM((nz, ny, 1, LANES), f32),
-        pltpu.VMEM((nx, groups, ny, 1, LANES), f32),
-        pltpu.VMEM((nx * groups - 1, ny, 1, LANES), f32),
+        pltpu.VMEM((nx, groups, 1, LANES), f32),
+        pltpu.VMEM((nz, nx, 1, LANES), f32),
+        pltpu.VMEM((ny, nx, 1, LANES), f32),
+        pltpu.VMEM((nx * groups - 1, 1, LANES), f32),
         pltpu.VMEM((count, LANES), f32),
         pltpu.VMEM((groups, 2 * nc, 8, lanes), bf16),
         pltpu.VMEM((2 * nc, 8, lanes), f32),

time: 39.5 us -> 36.5 us (0.924)
  Pallas kernels: 38.1 us -> 35.1 us
    pallas_call x1, Pallas kernels: 36.2 us -> 33.2 us  [run_exchange(): pl.pallas_call(functools.partial(exchange, ring, groups, nc), out_shape=(...]
where the time goes in v4:
time: 36.5 us; the launch traced here: 36.4 us
  Pallas kernels  35.1 us (96%)
  between operations  1.28 us (4%)
    pallas_call x1, Pallas kernels, run_exchange(): pl.pallas_call(functools.partial(exchange, ring, groups, nc), out_shape=(...  33.2 us
    pallas_call x1, Pallas kernels, run_combine(): pl.pallas_call(combine, grid=(2,), out_shape=(jax.ShapeDtypeStruct((rows,...  1.9 us

profile of v4, /device:TPU:1, one launch (start us, length us, event | category | flops | bytes accessed | tf_op | source)
XLA Modules:
  0.0 36.4 jit_solution(6664660294331890487)
XLA Ops:
  1.3 33.2 %exchange.1 = (bf16[512,512]{1,0:T(8,128)(2,1)S(1)}, bf16[512,1024]{1,0:T(8,128)(2,1)S(1)}) custom-call(s32[1,1]{1,0:T(1,128)} %bitcast.9.hole_hbm, f32[2,4,128]{2,1,0:T(4,128)} %vec_hbm.1, bf16[4,8,4096]{2,1,0:T(8,128)(2,1)} %bitcast.10, bf16[32,4096]{1,0:T(8,128)(2,1)} %bitcast.11, s32[3,256]{1,0:T(4,128)} %kpt_hbm.1, s32[3,512]{1,0:T(4,128)} %cell_hbm.1), custom_call_target="tpu_custom_call" | custom-call | tf_op jit(solution)/shard_map/exchange/pallas_call | solution.py:474
  34.5 1.9 %combine.1 = (f32[512,512]{1,0:T(8,128)}, f32[512,512]{1,0:T(8,128)}) custom-call(bf16[512,512]{1,0:T(8,128)(2,1)S(1)} %get-tuple-element.6.lhs, bf16[512,1024]{1,0:T(8,128)(2,1)S(1)} %get-tuple-element.7.table), custom_call_target="tpu_custom_call" | custom-call | tf_op jit(solution)/shard_map/combine/pallas_call | solution.py:505
